TPU v7x, 32 devices: a whole 2x2x4 slice. The times are simulated.
32 devices in a mesh: ctx: 8 (over z, core), head: 4 (over y, x).
Axes of the slice: x: 2, y: 2, z: 4, core: 2. Of those that a mesh axis runs over, the one named last changes fastest.
Arguments:
- q_latent: bfloat16 [1024, 128, 512], P('ctx', 'head'), may hold values from -4 to 4
- q_rope: bfloat16 [1024, 8192], P('ctx', 'head'), may hold values from -5 to 5
- latent: bfloat16 [1024, 512], P('ctx'), may hold values from -5 to 5
- key_rope: bfloat16 [1024, 64], P('ctx'), may hold values from -5 to 5
- out_grad: bfloat16 [1024, 128, 512], P('ctx', 'head'), may hold values from -5 to 5
- inputs: bfloat16 [1024, 7168], P('ctx', 'head'), may hold values from -5 to 5
- doc_ids: int32 [1024], replicated, may hold values from 0 to 7, never falling along the last dimension, each value on 1 to 256 neighbouring positions
Outputs:
- q_latent_grad: bfloat16 [1024, 128, 512], P('ctx', 'head')
- q_rope_grad: bfloat16 [1024, 8192], P('ctx', 'head')
- latent_grad: bfloat16 [1024, 512], P('ctx')
- key_rope_grad: bfloat16 [1024, 64], P('ctx')
- proj_grad: float32 [512, 7168], P('ctx', 'head')
Inputs may be any that keep to these rules, and one draw needn't show every extreme that they name: `doc_ids`: ids never fall along the sequence; each document has at most 256 positions.
All inputs are finite; a program needn't handle non-finite values.
Results may differ from a plain program's by a relative error of at most 0.0058.
Values may be sent and summed in bfloat16 or wider, within the bound.
No kernel may reach another device: no remote copies, remote signals or barrier semaphores. Data moves between devices by JAX's collectives and lax.ppermute only.
A program may use at most 128 MiB of HBM per device.

v0:
```python
import jax
import jax.numpy as jnp
from jax import lax
from jax.sharding import PartitionSpec as P

WIN_BLK = 3
softmax_scale = 192.0 ** (-0.5)


def passed_along(array, axis, by):
    peers = lax.axis_size(axis)
    pairs = [(i, i + by) for i in range(peers) if 0 <= i + by < peers]
    return lax.ppermute(array, axis, pairs)


def shards(q_latent, q_rope, latent, key_rope, out_grad, inputs, doc_ids):
    tok = latent.shape[0]
    heads_here = q_latent.shape[1]
    rope_width = key_rope.shape[1]
    lat_width = latent.shape[1]
    depth = WIN_BLK
    window = depth * tok
    rank = lax.axis_index("ctx")
    earlier = []
    for back in range(depth, 0, -1):
        earlier.append(passed_along((latent, key_rope), "ctx", back))
    keys_lat = jnp.concatenate([pair[0] for pair in earlier] + [latent], axis=0)
    keys_rope = jnp.concatenate([pair[1] for pair in earlier] + [key_rope], axis=0)
    start = rank * tok
    doc_pad = jnp.concatenate([jnp.full((window,), -1, jnp.int32), doc_ids], axis=0)
    key_doc = lax.dynamic_slice_in_dim(doc_pad, start, window + tok, 0)
    query_doc = lax.dynamic_slice_in_dim(doc_ids, start, tok, 0)
    qpos = jnp.arange(tok, dtype=jnp.int32)
    kpos = jnp.arange(window + tok, dtype=jnp.int32) - window
    allowed = (
        (kpos[None, :] <= qpos[:, None])
        & (qpos[:, None] - kpos[None, :] < window)
        & (key_doc[None, :] == query_doc[:, None])
    )
    qrope_heads = q_rope.reshape(tok, heads_here, rope_width)
    scores = (
        jnp.einsum("thj,kj->thk", q_latent, keys_lat, preferred_element_type=jnp.float32)
        + jnp.einsum("thr,kr->thk", qrope_heads, keys_rope, preferred_element_type=jnp.float32)
    ) * softmax_scale
    masked = jnp.where(allowed[:, None, :], scores, -jnp.inf)
    top = jnp.max(masked, axis=-1, keepdims=True)
    expo = jnp.exp(masked - top)
    probs = expo / jnp.sum(expo, axis=-1, keepdims=True)
    probs_low = probs.astype(jnp.bfloat16)
    merged = jnp.einsum("thk,kj->thj", probs_low, keys_lat, preferred_element_type=jnp.float32)
    delta = jnp.sum(out_grad * merged, axis=-1)
    dprob = jnp.einsum("thj,kj->thk", out_grad, keys_lat, preferred_element_type=jnp.float32)
    dscore = (probs * (dprob - delta[..., None]) * softmax_scale).astype(jnp.bfloat16)
    q_latent_grad = jnp.einsum(
        "thk,kj->thj", dscore, keys_lat, preferred_element_type=jnp.float32
    ).astype(jnp.bfloat16)
    q_rope_grad = jnp.einsum("thk,kr->thr", dscore, keys_rope, preferred_element_type=jnp.float32)
    q_rope_grad = q_rope_grad.reshape(tok, heads_here * rope_width).astype(jnp.bfloat16)
    part_lat = jnp.einsum(
        "thk,thj->kj", dscore, q_latent, preferred_element_type=jnp.float32
    ) + jnp.einsum("thk,thj->kj", probs_low, out_grad, preferred_element_type=jnp.float32)
    part_rope = jnp.einsum("thk,thr->kr", dscore, qrope_heads, preferred_element_type=jnp.float32)
    blocks_lat = part_lat.reshape(depth + 1, tok, lat_width)
    blocks_rope = part_rope.reshape(depth + 1, tok, rope_width)
    share_lat, share_rope = (
        lax.psum_scatter(blocks_lat, "head", scatter_dimension=1, tiled=True),
        lax.psum_scatter(blocks_rope, "head", scatter_dimension=1, tiled=True),
    )
    own_lat = share_lat[depth]
    own_rope = share_rope[depth]
    for back in range(1, depth + 1):
        got_lat, got_rope = passed_along(
            (share_lat[depth - back], share_rope[depth - back]), "ctx", -back
        )
        own_lat = own_lat + got_lat
        own_rope = own_rope + got_rope
    latent_grad, key_rope_grad = (
        lax.all_gather(own_lat.astype(jnp.bfloat16), "head", axis=0, tiled=True),
        lax.all_gather(own_rope.astype(jnp.bfloat16), "head", axis=0, tiled=True),
    )
    proj_grad = lax.psum_scatter(
        lax.dot_general(
            latent_grad, inputs, (((0,), (0,)), ((), ())), preferred_element_type=jnp.float32
        ),
        "ctx",
        scatter_dimension=0,
        tiled=True,
    )
    return (q_latent_grad, q_rope_grad, latent_grad, key_rope_grad, proj_grad)


def solution(mesh):
    placed = (
        P("ctx", "head", None),
        P("ctx", "head"),
        P("ctx", None),
        P("ctx", None),
        P("ctx", "head", None),
        P("ctx", "head"),
        P(),
    )
    return jax.shard_map(
        shards,
        mesh=mesh,
        in_specs=placed,
        out_specs=(
            P("ctx", "head", None),
            P("ctx", "head"),
            P("ctx", None),
            P("ctx", None),
            P("ctx", "head"),
        ),
        check_vma=False,
    )
```

profile of v0, /device:TPU:0, one launch (start us, length us, event | category | flops | bytes accessed | tf_op | source)
XLA Modules:
  0.0 199.9 jit_solution(8502988981172908835)
XLA Ops:
  7.2 4.5 %collective-permute-start.3 = (bf16[128,64]{0,1:T(8,128)(2,1)}, bf16[128,64]{0,1:T(8,128)(2,1)S(1)}, u32[]{:S(2)}, u32[]{:S(2)}) collective-permute-start(bf16[128,64]{0,1:T(8,128)(2,1)} %param.10), channel_id=1, source_target_pairs={{0,12},{4,16},{8,20},{12,24},{16,28},{1,13},{5,17},{9,21},{13,25},... | collective-permute-start | bytes 49160 | tf_op jit(solution)/shard_map/ppermute | solution.py:13
  11.8 3.5 %collective-permute-start.4 = (bf16[128,64]{0,1:T(8,128)(2,1)}, bf16[128,64]{0,1:T(8,128)(2,1)S(1)}, u32[]{:S(2)}, u32[]{:S(2)}) collective-permute-start(bf16[128,64]{0,1:T(8,128)(2,1)} %param.10), channel_id=1, source_target_pairs={{0,8},{4,12},{8,16},{12,20},{16,24},{20,28},{1,9},{5,13},{9,17},{1... | collective-permute-start | bytes 49160 | tf_op jit(solution)/shard_map/ppermute | solution.py:13
  15.3 3.3 %collective-permute-start.5 = (bf16[128,64]{0,1:T(8,128)(2,1)}, bf16[128,64]{0,1:T(8,128)(2,1)S(1)}, u32[]{:S(2)}, u32[]{:S(2)}) collective-permute-start(bf16[128,64]{0,1:T(8,128)(2,1)} %param.10), channel_id=1, source_target_pairs={{0,4},{4,8},{8,12},{12,16},{16,20},{20,24},{24,28},{1,5},{5,9},{9,... | collective-permute-start | bytes 49160 | tf_op jit(solution)/shard_map/ppermute | solution.py:13
  18.6 1.8 collective-permute-start
  20.4 1.7 collective-permute-start.1
  22.1 0.8 pad_dynamic-slice_fusion
  22.9 0.8 dynamic_slice.7
  23.7 0.2 fusion.34
  23.9 1.3 copy.27
  25.2 2.3 %collective-permute-start.2 = (bf16[128,512]{1,0:T(8,128)(2,1)}, bf16[128,512]{1,0:T(8,128)(2,1)S(1)}, u32[]{:S(2)}, u32[]{:S(2)}) collective-permute-start(bf16[128,512]{1,0:T(8,128)(2,1)} %param.9), channel_id=1, source_target_pairs={{0,4},{4,8},{8,12},{12,16},{16,20},{20,24},{24,28},{1,5},{5,9},{9,... | collective-permute-start | bytes 393224 | tf_op jit(solution)/shard_map/ppermute | solution.py:13
  27.5 2.0 fusion.41
  29.5 9.6 %fusion.7 = (f32[128,32]{0,1:T(8,128)S(1)}, f32[512,128,32]{1,0,2:T(8,128)S(1)}) fusion(pred[128,512]{0,1:T(8,128)(4,1)S(1)} %fusion.34, f32[512,128,32]{1,0,2:T(8,128)S(1)} %fusion.41, bf16[128,32,512]{2,1,0:T(8,128)(2,1)} %param.7, bf16[128,512]{1,0:T(8,128)(2,1)S(1)} %copy-done.3, bf16[128,512]{1,0:T(8,128)(2,1)S(1)} %collective-permute-done.2, ...), kind=kOutput, calls=%fused_computation.14 | convolution fusion | flops 2157965312 | bytes 21577728 | tf_op jit(solution)/shard_map/thj,kj->thk/dot_general | solution.py:42
  39.1 1.6 fusion.9
  40.8 3.6 %copy-done.5 = bf16[128,32,512]{2,1,0:T(8,128)(2,1)S(1)} copy-done((bf16[128,32,512]{2,1,0:T(8,128)(2,1)S(1)}, bf16[128,32,512]{2,1,0:T(8,128)(2,1)}, u32[]{:S(2)}) %copy-start.5) | copy-done | bytes 4194328
  44.4 7.6 %fusion.22 = f32[512,512]{1,0:T(8,128)S(1)} fusion(bf16[128,32,512]{2,1,0:T(8,128)(2,1)S(1)} %copy-done.5, f32[512,128,32]{1,0,2:T(8,128)S(1)} %get-tuple-element.22, f32[128,32]{0,1:T(8,128)S(1)} %fusion.9, f32[128,32]{0,1:T(8,128)S(1)} %get-tuple-element.21, pred[128,512]{0,1:T(8,128)(4,1)S(1)} %fusion.34), kind=kOutput, calls=%fused_computation.28 | convolution fusion | flops 2155872256 | bytes 13729792 | tf_op jit(solution)/shard_map/thk,thj->kj/dot_general | solution.py:61
  52.0 7.4 %multiply_reduce_fusion = f32[128,32]{0,1:T(8,128)S(1)} fusion(bf16[128,32,512]{2,1,0:T(8,128)(2,1)S(1)} %copy-done.5, bf16[128,512]{1,0:T(8,128)(2,1)S(1)} %copy-done.3, bf16[128,512]{1,0:T(8,128)(2,1)S(1)} %collective-permute-done.2, bf16[128,512]{1,0:T(8,128)(2,1)S(1)} %collective-permute-done.1, bf16[128,512]{1,0:T(8,128)(2,1)S(1)} %collective-permute-done, ...), kind=kOutput, calls=%fused_computation.11 | convolution fusion | flops 2164256768 | bytes 13221888 | tf_op jit(solution)/shard_map/thk,kj->thj/dot_general | solution.py:50
  59.4 10.1 %fusion.6 = (bf16[128,32,512]{0,2,1:T(8,128)(2,1)S(1)}, f32[512,128,32]{1,0,2:T(8,128)}) fusion(f32[128,32]{0,1:T(8,128)S(1)} %multiply_reduce_fusion, f32[128,32]{0,1:T(8,128)S(1)} %fusion.9, f32[128,32]{0,1:T(8,128)S(1)} %get-tuple-element.21, f32[512,128,32]{1,0,2:T(8,128)S(1)} %get-tuple-element.22, pred[128,512]{0,1:T(8,128)(4,1)S(1)} %fusion.34, ...), kind=kOutput, calls=%fused_computation.9 | convolution fusion | flops 2164260864 | bytes 25804800 | tf_op jit(solution)/shard_map/thj,kj->thk/dot_general | solution.py:52
  69.6 2.0 %copy-done.2 = bf16[128,32,512]{0,2,1:T(8,128)(2,1)} copy-done((bf16[128,32,512]{0,2,1:T(8,128)(2,1)}, bf16[128,32,512]{0,2,1:T(8,128)(2,1)S(1)}, u32[]{:S(2)}) %copy-start.2) | copy-done | bytes 4194328
  71.6 8.3 %fusion.30 = f32[512,512]{1,0:T(8,128)} fusion(f32[512,512]{1,0:T(8,128)S(1)} %fusion.22, bf16[128,32,512]{0,2,1:T(8,128)(2,1)S(1)} %get-tuple-element.23, bf16[128,32,512]{2,1,0:T(8,128)(2,1)} %param.7), kind=kOutput, calls=%fused_computation.30 | convolution fusion | flops 2147745792 | bytes 10485760 | tf_op jit(solution)/shard_map/thk,thj->kj/dot_general | solution.py:59
  79.9 0.0 reduce-scatter.6.cloned.1.call-start
  80.0 0.2 fusion.36
  80.2 8.6 %fusion.2 = bf16[512,32,128]{2,0,1:T(8,128)(2,1)} fusion(f32[512,128,32]{1,0,2:T(8,128)} %get-tuple-element.24, f32[512,128,32]{1,0,2:T(8,128)} %copy-done.1, f32[32,128]{1,0:T(8,128)S(1)} %bitcast.120, f32[32,128]{1,0:T(8,128)S(1)} %bitcast.119, f32[32,128]{1,0:T(8,128)S(1)} %bitcast.118, pred[512,128]{1,0:T(8,128)(4,1)S(1)} %fusion.36), kind=kLoop, calls=%fused_computation.3 | loop fusion | flops 14680064 | bytes 21086208 | tf_op jit(solution)/shard_map/convert_element_type | solution.py:53
  88.8 19.6 %reduce-scatter.4.cloned.1.call-done = f32[4,32,512]{2,1,0:T(8,128)} async-done(((f32[4,128,512]{2,1,0:T(8,128)}), f32[4,32,512]{2,1,0:T(8,128)}) %reduce-scatter.4.cloned.1.call-update) | async-done | bytes 262160 | tf_op jit(solution)/shard_map/reduce_scatter | solution.py:66
  108.3 0.9 slice_bitcast_fusion.2
  109.2 1.3 collective-permute-start.6
  110.5 1.3 collective-permute-start.7
  111.8 1.3 collective-permute-start.8
  113.1 4.1 %convolution_bitcast_fusion = f32[4,128,64]{2,1,0:T(8,128)} fusion(bf16[4,128,32,128]{3,1,0,2:T(8,128)(2,1)} %bitcast.113, bf16[128,32,64,1]{0,2,3,1:T(8,128)(2,1)S(1)} %bitcast.115), kind=kOutput, calls=%fused_computation.32 | convolution fusion | flops 268435456 | bytes 4849664 | tf_op jit(solution)/shard_map/thk,thr->kr/dot_general | solution.py:62
  117.3 0.0 reduce-scatter.8.cloned.1.call-start
  117.4 0.1 collective-permute-done.7
  117.4 1.4 collective-permute-done.8
  118.8 0.9 fusion.40
  119.7 8.4 %all_gather.6 = bf16[128,512]{1,0:T(8,128)(2,1)S(1)} all-gather(bf16[32,512]{1,0:T(8,128)(2,1)S(1)} %fusion.40), channel_id=1, replica_groups=mesh['ctx'=8,'head'=4] {'head'}, dimensions={0}, use_global_device_ids=true | all-gather | bytes 163840 | tf_op jit(solution)/shard_map/all_gather | solution.py:78
  128.1 2.5 %fusion.50 = f32[512,1792]{1,0:T(8,128)} fusion(bf16[128,512]{1,0:T(8,128)(2,1)S(1)} %all_gather.6, bf16[128,1792]{1,0:T(8,128)(2,1)S(1)} %copy-done), kind=kOutput, calls=%fused_computation.64 | convolution fusion | flops 234881024 | bytes 4259840 | tf_op jit(solution)/shard_map/dot_general | solution.py:82
  130.6 6.5 %convolution_convert_fusion = bf16[128,32,512]{2,0,1:T(8,128)(2,1)} fusion(bf16[128,32,512]{0,2,1:T(8,128)(2,1)} %copy-done.2, bf16[128,512]{1,0:T(8,128)(2,1)S(1)} %copy-done.3, bf16[128,512]{1,0:T(8,128)(2,1)S(1)} %collective-permute-done.2, bf16[128,512]{1,0:T(8,128)(2,1)S(1)} %collective-permute-done.1, bf16[128,512]{1,0:T(8,128)(2,1)S(1)} %collective-permute-done), kind=kOutput, calls=%fused_computation.25 | convolution fusion | flops 2151677952 | bytes 8912896 | tf_op jit(solution)/shard_map/thk,kj->thj/dot_general | solution.py:54
  137.1 7.4 %reduce-scatter.6.cloned.1.call-done = f32[4,32,64]{2,1,0:T(8,128)} async-done(((f32[4,128,64]{2,1,0:T(8,128)}), f32[4,32,64]{2,1,0:T(8,128)}) %reduce-scatter.6.cloned.1.call-update) | async-done | bytes 32784 | tf_op jit(solution)/shard_map/reduce_scatter | solution.py:67
  144.5 0.8 slice_bitcast_fusion.6
  145.3 1.3 collective-permute-start.10
  146.6 1.3 collective-permute-start.11
  147.9 1.6 collective-permute-start.9
  149.5 3.0 %convolution_convert_fusion.1 = bf16[128,32,64]{0,2,1:T(8,128)(2,1)S(1)} fusion(bf16[128,32,512]{0,2,1:T(8,128)(2,1)} %copy-done.2, bf16[128,64]{0,1:T(8,128)(2,1)S(1)} %copy-done.4, bf16[128,64]{0,1:T(8,128)(2,1)S(1)} %collective-permute-done.5, bf16[128,64]{0,1:T(8,128)(2,1)S(1)} %collective-permute-done.4, bf16[128,64]{0,1:T(8,128)(2,1)S(1)} %collective-permute-done.3), kind=kOutput, calls=%fused_computation.31 | convolution fusion | flops 268959744 | bytes 4784128 | tf_op jit(solution)/shard_map/thk,kr->thr/dot_general | solution.py:57
  152.5 6.9 %copy.36 = bf16[128,32,512]{2,1,0:T(8,128)(2,1)} copy(bf16[128,32,512]{2,0,1:T(8,128)(2,1)} %convolution_convert_fusion) | data formatting | bytes 8388608
  159.4 1.0 copy.37
  160.4 0.7 fusion.45
  161.1 8.2 %all_gather.7 = bf16[128,64]{1,0:T(8,128)(2,1)S(1)} all-gather(bf16[32,64]{1,0:T(8,128)(2,1)S(1)} %fusion.45), channel_id=1, replica_groups=mesh['ctx'=8,'head'=4] {'head'}, dimensions={0}, use_global_device_ids=true | all-gather | bytes 20480 | tf_op jit(solution)/shard_map/all_gather | solution.py:79
  169.3 0.7 copy.38
  170.0 22.7 %reduce-scatter.8.cloned.1.call-done = f32[64,1792]{1,0:T(8,128)} async-done(((f32[512,1792]{1,0:T(8,128)}), f32[64,1792]{1,0:T(8,128)}) %reduce-scatter.8.cloned.1.call-update) | async-done | bytes 458768 | tf_op jit(solution)/shard_map/reduce_scatter | solution.py:81
  192.7 0.7 copy.66
  (24 shorter events, 0.1 us)
Async XLA Ops:
  7.2 120.9 %copy-start = (bf16[128,1792]{1,0:T(8,128)(2,1)S(1)}, bf16[128,1792]{1,0:T(8,128)(2,1)}, u32[]{:S(2)}) copy-start(bf16[128,1792]{1,0:T(8,128)(2,1)} %param.12) | copy-start | bytes 1376260
  7.2 22.3 %copy-start.3 = (bf16[128,512]{1,0:T(8,128)(2,1)S(1)}, bf16[128,512]{1,0:T(8,128)(2,1)}, u32[]{:S(2)}) copy-start(bf16[128,512]{1,0:T(8,128)(2,1)} %param.9) | copy-start | bytes 393220
  7.2 101.1 %reduce-scatter.4.cloned.1.call-start = ((), (), s32[]{:S(2)}) async-start(), calls=%async_computation.3 | async-start | bytes 1310720 | tf_op jit(solution)/shard_map/reduce_scatter | solution.py:66
  7.2 18.0 %collective-permute-start.3 = (bf16[128,64]{0,1:T(8,128)(2,1)}, bf16[128,64]{0,1:T(8,128)(2,1)S(1)}, u32[]{:S(2)}, u32[]{:S(2)}) collective-permute-start(bf16[128,64]{0,1:T(8,128)(2,1)} %param.10), channel_id=1, source_target_pairs={{0,12},{4,16},{8,20},{12,24},{16,28},{1,13},{5,17},{9,21},{13,25},... | collective-permute-start | bytes 49160 | tf_op jit(solution)/shard_map/ppermute | solution.py:13
  11.8 15.7 %collective-permute-start.4 = (bf16[128,64]{0,1:T(8,128)(2,1)}, bf16[128,64]{0,1:T(8,128)(2,1)S(1)}, u32[]{:S(2)}, u32[]{:S(2)}) collective-permute-start(bf16[128,64]{0,1:T(8,128)(2,1)} %param.10), channel_id=1, source_target_pairs={{0,8},{4,12},{8,16},{12,20},{16,24},{20,28},{1,9},{5,13},{9,17},{1... | collective-permute-start | bytes 49160 | tf_op jit(solution)/shard_map/ppermute | solution.py:13
  15.3 12.2 %collective-permute-start.5 = (bf16[128,64]{0,1:T(8,128)(2,1)}, bf16[128,64]{0,1:T(8,128)(2,1)S(1)}, u32[]{:S(2)}, u32[]{:S(2)}) collective-permute-start(bf16[128,64]{0,1:T(8,128)(2,1)} %param.10), channel_id=1, source_target_pairs={{0,4},{4,8},{8,12},{12,16},{16,20},{20,24},{24,28},{1,5},{5,9},{9,... | collective-permute-start | bytes 49160 | tf_op jit(solution)/shard_map/ppermute | solution.py:13
  18.6 10.9 %collective-permute-start = (bf16[128,512]{1,0:T(8,128)(2,1)}, bf16[128,512]{1,0:T(8,128)(2,1)S(1)}, u32[]{:S(2)}, u32[]{:S(2)}) collective-permute-start(bf16[128,512]{1,0:T(8,128)(2,1)} %param.9), channel_id=1, source_target_pairs={{0,12},{4,16},{8,20},{12,24},{16,28},{1,13},{5,17},{9,21},{13,25},... | collective-permute-start | bytes 393224 | tf_op jit(solution)/shard_map/ppermute | solution.py:13
  20.4 9.1 %collective-permute-start.1 = (bf16[128,512]{1,0:T(8,128)(2,1)}, bf16[128,512]{1,0:T(8,128)(2,1)S(1)}, u32[]{:S(2)}, u32[]{:S(2)}) collective-permute-start(bf16[128,512]{1,0:T(8,128)(2,1)} %param.9), channel_id=1, source_target_pairs={{0,8},{4,12},{8,16},{12,20},{16,24},{20,28},{1,9},{5,13},{9,17},{1... | collective-permute-start | bytes 393224 | tf_op jit(solution)/shard_map/ppermute | solution.py:13
  25.2 4.3 %collective-permute-start.2 = (bf16[128,512]{1,0:T(8,128)(2,1)}, bf16[128,512]{1,0:T(8,128)(2,1)S(1)}, u32[]{:S(2)}, u32[]{:S(2)}) collective-permute-start(bf16[128,512]{1,0:T(8,128)(2,1)} %param.9), channel_id=1, source_target_pairs={{0,4},{4,8},{8,12},{12,16},{16,20},{20,24},{24,28},{1,5},{5,9},{9,... | collective-permute-start | bytes 393224 | tf_op jit(solution)/shard_map/ppermute | solution.py:13
  39.1 20.3 %copy-start.1 = (f32[512,128,32]{1,0,2:T(8,128)}, f32[512,128,32]{1,0,2:T(8,128)S(1)}, u32[]{:S(2)}) copy-start(f32[512,128,32]{1,0,2:T(8,128)S(1)} %get-tuple-element.22) | copy-start | bytes 25165828
  39.1 5.2 %copy-start.5 = (bf16[128,32,512]{2,1,0:T(8,128)(2,1)S(1)}, bf16[128,32,512]{2,1,0:T(8,128)(2,1)}, u32[]{:S(2)}) copy-start(bf16[128,32,512]{2,1,0:T(8,128)(2,1)} %param.11) | copy-start | bytes 12582916
  69.5 2.0 %copy-start.2 = (bf16[128,32,512]{0,2,1:T(8,128)(2,1)}, bf16[128,32,512]{0,2,1:T(8,128)(2,1)S(1)}, u32[]{:S(2)}) copy-start(bf16[128,32,512]{0,2,1:T(8,128)(2,1)S(1)} %get-tuple-element.23) | copy-start | bytes 12582916
  79.9 64.6 %reduce-scatter.6.cloned.1.call-start = ((), (), s32[]{:S(2)}) async-start(), calls=%async_computation.4 | async-start | bytes 327680 | tf_op jit(solution)/shard_map/reduce_scatter | solution.py:67
  109.2 8.1 %collective-permute-start.6 = (f32[32,512]{1,0:T(8,128)S(1)}, f32[32,512]{1,0:T(8,128)S(1)}, u32[]{:S(2)}, u32[]{:S(2)}) collective-permute-start(f32[32,512]{1,0:T(8,128)S(1)} %get-tuple-element.15), channel_id=1, source_target_pairs={{4,0},{8,4},{12,8},{16,12},{20,16},{24,20},{28,24},{5,1},{9,5},{13... | collective-permute-start | bytes 196616 | tf_op jit(solution)/shard_map/ppermute | solution.py:13
  110.5 6.9 %collective-permute-start.7 = (f32[32,512]{1,0:T(8,128)S(1)}, f32[32,512]{1,0:T(8,128)S(1)}, u32[]{:S(2)}, u32[]{:S(2)}) collective-permute-start(f32[32,512]{1,0:T(8,128)S(1)} %get-tuple-element.17), channel_id=1, source_target_pairs={{8,0},{12,4},{16,8},{20,12},{24,16},{28,20},{9,1},{13,5},{17,9},{2... | collective-permute-start | bytes 196616 | tf_op jit(solution)/shard_map/ppermute | solution.py:13
  111.8 6.9 %collective-permute-start.8 = (f32[32,512]{1,0:T(8,128)S(1)}, f32[32,512]{1,0:T(8,128)S(1)}, u32[]{:S(2)}, u32[]{:S(2)}) collective-permute-start(f32[32,512]{1,0:T(8,128)S(1)} %get-tuple-element.16), channel_id=1, source_target_pairs={{12,0},{16,4},{20,8},{24,12},{28,16},{13,1},{17,5},{21,9},{25,13},... | collective-permute-start | bytes 196616 | tf_op jit(solution)/shard_map/ppermute | solution.py:13
  117.3 75.4 %reduce-scatter.8.cloned.1.call-start = ((), (), s32[]{:S(2)}) async-start(), calls=%async_computation.5 | async-start | bytes 4128768 | tf_op jit(solution)/shard_map/reduce_scatter | solution.py:81
  128.1 21.4 %copy-start.4 = (bf16[128,64]{0,1:T(8,128)(2,1)S(1)}, bf16[128,64]{0,1:T(8,128)(2,1)}, u32[]{:S(2)}) copy-start(bf16[128,64]{0,1:T(8,128)(2,1)} %param.10) | copy-start | bytes 49156
  145.3 15.1 %collective-permute-start.10 = (f32[32,64]{1,0:T(8,128)S(1)}, f32[32,64]{1,0:T(8,128)S(1)}, u32[]{:S(2)}, u32[]{:S(2)}) collective-permute-start(f32[32,64]{1,0:T(8,128)S(1)} %get-tuple-element.20), channel_id=1, source_target_pairs={{8,0},{12,4},{16,8},{20,12},{24,16},{28,20},{9,1},{13,5},{17,9},{2... | collective-permute-start | bytes 24584 | tf_op jit(solution)/shard_map/ppermute | solution.py:13
  146.6 13.8 %collective-permute-start.11 = (f32[32,64]{1,0:T(8,128)S(1)}, f32[32,64]{1,0:T(8,128)S(1)}, u32[]{:S(2)}, u32[]{:S(2)}) collective-permute-start(f32[32,64]{1,0:T(8,128)S(1)} %get-tuple-element.19), channel_id=1, source_target_pairs={{12,0},{16,4},{20,8},{24,12},{28,16},{13,1},{17,5},{21,9},{25,13},... | collective-permute-start | bytes 24584 | tf_op jit(solution)/shard_map/ppermute | solution.py:13
  147.9 12.5 %collective-permute-start.9 = (f32[32,64]{1,0:T(8,128)S(1)}, f32[32,64]{1,0:T(8,128)S(1)}, u32[]{:S(2)}, u32[]{:S(2)}) collective-permute-start(f32[32,64]{1,0:T(8,128)S(1)} %get-tuple-element.18), channel_id=1, source_target_pairs={{4,0},{8,4},{12,8},{16,12},{20,16},{24,20},{28,24},{5,1},{9,5},{13... | collective-permute-start | bytes 24584 | tf_op jit(solution)/shard_map/ppermute | solution.py:13
Sparse Core Ops, SparseCore 0:
  80.0 28.2 reduce-scatter.3
  117.4 27.0 reduce-scatter.5
  147.4 45.2 reduce-scatter.7
where the time goes:
time: 201 us; the launch traced here: 200 us
  matrix products  61.2 us (30%)
  waiting for transfers between devices  51.3 us (26%)
  starting transfers between devices  25.2 us (13%)
  local copies, waits for them, and re-layouts  18.6 us (9%)
  blocking collectives  16.6 us (8%)
  between operations  14 us (7%)
  other arithmetic  13 us (6%)
    ppermute x12, starting transfers between devices, passed_along(): return lax.ppermute(array, axis, pairs)  25.1 us
    reduce_scatter x1, waiting for transfers between devices, shards(): lax.psum_scatter(lax.dot_general(latent_grad, inputs, (((0,), (0,)), ((),...  22.7 us
    reduce_scatter x1, waiting for transfers between devices, shards(): lax.psum_scatter(blocks_lat, 'head', scatter_dimension=1, tiled=True)  19.6 us
    unnamed x17, local copies, waits for them, and re-layouts  16.2 us
    dot_general x1, matrix products, shards(): jnp.einsum('thj,kj->thk', out_grad, keys_lat, preferred_element_type=jnp....  10.1 us
    dot_general x1, matrix products, shards(): jnp.einsum('thj,kj->thk', q_latent, keys_lat, preferred_element_type=jnp....  9.59 us
    convert_element_type x1, other arithmetic, shards(): (probs * (dprob - delta[..., None]) * softmax_scale).astype(jnp.bfloat16)  8.59 us
    all_gather x1, blocking collectives, shards(): lax.all_gather(own_lat.astype(jnp.bfloat16), 'head', axis=0, tiled=True)  8.41 us
  transfers between devices with their start and end apart: 15, of which 5 were waited for; matrix products, arithmetic and copies ran while one was open for 20% of the time, Pallas kernels for 0%

commit v1 on v0

--- a/solution.py
+++ b/solution.py
@@ -75,7 +75,12 @@
         own_lat = own_lat + got_lat
         own_rope = own_rope + got_rope
     latent_grad, key_rope_grad = (
-        lax.all_gather(own_lat.astype(jnp.bfloat16), "head", axis=0, tiled=True),
+        jnp.concatenate(
+            lax.all_to_all(
+                jnp.stack([own_lat.astype(jnp.bfloat16)] * lax.axis_size("head")), "head", 0, 0
+            ),
+            0,
+        ),
         lax.all_gather(own_rope.astype(jnp.bfloat16), "head", axis=0, tiled=True),
     )
     proj_grad = lax.psum_scatter(

time: 201 us -> 216 us (1.075)
  waiting for transfers between devices: 51.3 us -> 70.5 us
  blocking collectives: 16.6 us -> 8.16 us
  starting transfers between devices: 25.2 us -> 28.6 us
    reduce_scatter x1, waiting for transfers between devices: 7.45 us -> 18.6 us  [shards(): lax.psum_scatter(blocks_rope, 'head', scatter_dimension=1, tiled=True)]
    reduce_scatter x1, waiting for transfers between devices: 19.6 us -> 28.2 us  [shards(): lax.psum_scatter(blocks_lat, 'head', scatter_dimension=1, tiled=True)]
    all_gather x1 -> x0, blocking collectives: 8.41 us -> none  [shards(): lax.all_gather(own_lat.astype(jnp.bfloat16), 'head', axis=0, tiled=True)]
    all_to_all x0 -> x1, starting transfers between devices: none -> 3.33 us  [shards(): lax.all_to_all(jnp.stack([own_lat.astype(jnp.bfloat16)] * lax.axis_size('...]
  transfers between devices with their start and end apart: 15 -> 16, of which waited for: 5 -> 4; matrix products, arithmetic and copies ran while one was open for 20% -> 19% of each run, Pallas kernels for 0% -> 0%
where the time goes in v1:
time: 216 us; the launch traced here: 215 us
  waiting for transfers between devices  70.5 us (33%)
  matrix products  61.2 us (28%)
  starting transfers between devices  28.6 us (13%)
  local copies, waits for them, and re-layouts  19.3 us (9%)
  between operations  14 us (6%)
  other arithmetic  13.1 us (6%)
  blocking collectives  8.16 us (4%)
    reduce_scatter x1, waiting for transfers between devices, shards(): lax.psum_scatter(blocks_lat, 'head', scatter_dimension=1, tiled=True)  28.2 us
    ppermute x12, starting transfers between devices, passed_along(): return lax.ppermute(array, axis, pairs)  25.1 us
    reduce_scatter x1, waiting for transfers between devices, shards(): lax.psum_scatter(lax.dot_general(latent_grad, inputs, (((0,), (0,)), ((),...  22.7 us
    reduce_scatter x1, waiting for transfers between devices, shards(): lax.psum_scatter(blocks_rope, 'head', scatter_dimension=1, tiled=True)  18.6 us
    unnamed x17, local copies, waits for them, and re-layouts  16.2 us
    dot_general x1, matrix products, shards(): jnp.einsum('thj,kj->thk', out_grad, keys_lat, preferred_element_type=jnp....  10.1 us
    dot_general x1, matrix products, shards(): jnp.einsum('thj,kj->thk', q_latent, keys_lat, preferred_element_type=jnp....  9.59 us
    convert_element_type x1, other arithmetic, shards(): (probs * (dprob - delta[..., None]) * softmax_scale).astype(jnp.bfloat16)  8.71 us
  transfers between devices with their start and end apart: 16, of which 4 were waited for; matrix products, arithmetic and copies ran while one was open for 19% of the time, Pallas kernels for 0%

profile of v1, /device:TPU:0, one launch (start us, length us, event | category | flops | bytes accessed | tf_op | source)
XLA Modules:
  0.0 214.8 jit_solution(594858309032413089)
XLA Ops:
  7.2 4.5 %collective-permute-start.3 = (bf16[128,64]{0,1:T(8,128)(2,1)}, bf16[128,64]{0,1:T(8,128)(2,1)S(1)}, u32[]{:S(2)}, u32[]{:S(2)}) collective-permute-start(bf16[128,64]{0,1:T(8,128)(2,1)} %param.10), channel_id=1, source_target_pairs={{0,12},{4,16},{8,20},{12,24},{16,28},{1,13},{5,17},{9,21},{13,25},... | collective-permute-start | bytes 49160 | tf_op jit(solution)/shard_map/ppermute | solution.py:13
  11.8 3.5 %collective-permute-start.4 = (bf16[128,64]{0,1:T(8,128)(2,1)}, bf16[128,64]{0,1:T(8,128)(2,1)S(1)}, u32[]{:S(2)}, u32[]{:S(2)}) collective-permute-start(bf16[128,64]{0,1:T(8,128)(2,1)} %param.10), channel_id=1, source_target_pairs={{0,8},{4,12},{8,16},{12,20},{16,24},{20,28},{1,9},{5,13},{9,17},{1... | collective-permute-start | bytes 49160 | tf_op jit(solution)/shard_map/ppermute | solution.py:13
  15.3 3.3 %collective-permute-start.5 = (bf16[128,64]{0,1:T(8,128)(2,1)}, bf16[128,64]{0,1:T(8,128)(2,1)S(1)}, u32[]{:S(2)}, u32[]{:S(2)}) collective-permute-start(bf16[128,64]{0,1:T(8,128)(2,1)} %param.10), channel_id=1, source_target_pairs={{0,4},{4,8},{8,12},{12,16},{16,20},{20,24},{24,28},{1,5},{5,9},{9,... | collective-permute-start | bytes 49160 | tf_op jit(solution)/shard_map/ppermute | solution.py:13
  18.6 1.8 collective-permute-start
  20.4 1.7 collective-permute-start.1
  22.1 0.8 pad_dynamic-slice_fusion
  22.9 0.8 dynamic_slice.7
  23.7 0.2 fusion.34
  23.9 1.3 copy.27
  25.2 2.3 %collective-permute-start.2 = (bf16[128,512]{1,0:T(8,128)(2,1)}, bf16[128,512]{1,0:T(8,128)(2,1)S(1)}, u32[]{:S(2)}, u32[]{:S(2)}) collective-permute-start(bf16[128,512]{1,0:T(8,128)(2,1)} %param.9), channel_id=1, source_target_pairs={{0,4},{4,8},{8,12},{12,16},{16,20},{20,24},{24,28},{1,5},{5,9},{9,... | collective-permute-start | bytes 393224 | tf_op jit(solution)/shard_map/ppermute | solution.py:13
  27.5 2.0 fusion.41
  29.5 9.6 %fusion.7 = (f32[128,32]{0,1:T(8,128)S(1)}, f32[512,128,32]{1,0,2:T(8,128)S(1)}) fusion(pred[128,512]{0,1:T(8,128)(4,1)S(1)} %fusion.34, f32[512,128,32]{1,0,2:T(8,128)S(1)} %fusion.41, bf16[128,32,512]{2,1,0:T(8,128)(2,1)} %param.7, bf16[128,512]{1,0:T(8,128)(2,1)S(1)} %copy-done.3, bf16[128,512]{1,0:T(8,128)(2,1)S(1)} %collective-permute-done.2, ...), kind=kOutput, calls=%fused_computation.14 | convolution fusion | flops 2157965312 | bytes 21577728 | tf_op jit(solution)/shard_map/thj,kj->thk/dot_general | solution.py:42
  39.1 1.6 fusion.9
  40.8 3.6 %copy-done.5 = bf16[128,32,512]{2,1,0:T(8,128)(2,1)S(1)} copy-done((bf16[128,32,512]{2,1,0:T(8,128)(2,1)S(1)}, bf16[128,32,512]{2,1,0:T(8,128)(2,1)}, u32[]{:S(2)}) %copy-start.5) | copy-done | bytes 4194328
  44.4 7.6 %fusion.22 = f32[512,512]{1,0:T(8,128)S(1)} fusion(bf16[128,32,512]{2,1,0:T(8,128)(2,1)S(1)} %copy-done.5, f32[512,128,32]{1,0,2:T(8,128)S(1)} %get-tuple-element.22, f32[128,32]{0,1:T(8,128)S(1)} %fusion.9, f32[128,32]{0,1:T(8,128)S(1)} %get-tuple-element.21, pred[128,512]{0,1:T(8,128)(4,1)S(1)} %fusion.34), kind=kOutput, calls=%fused_computation.28 | convolution fusion | flops 2155872256 | bytes 13729792 | tf_op jit(solution)/shard_map/thk,thj->kj/dot_general | solution.py:61
  52.0 7.4 %multiply_reduce_fusion = f32[128,32]{0,1:T(8,128)S(1)} fusion(bf16[128,32,512]{2,1,0:T(8,128)(2,1)S(1)} %copy-done.5, bf16[128,512]{1,0:T(8,128)(2,1)S(1)} %copy-done.3, bf16[128,512]{1,0:T(8,128)(2,1)S(1)} %collective-permute-done.2, bf16[128,512]{1,0:T(8,128)(2,1)S(1)} %collective-permute-done.1, bf16[128,512]{1,0:T(8,128)(2,1)S(1)} %collective-permute-done, ...), kind=kOutput, calls=%fused_computation.11 | convolution fusion | flops 2164256768 | bytes 13221888 | tf_op jit(solution)/shard_map/thk,kj->thj/dot_general | solution.py:50
  59.4 10.1 %fusion.6 = (bf16[128,32,512]{0,2,1:T(8,128)(2,1)S(1)}, f32[512,128,32]{1,0,2:T(8,128)}) fusion(f32[128,32]{0,1:T(8,128)S(1)} %multiply_reduce_fusion, f32[128,32]{0,1:T(8,128)S(1)} %fusion.9, f32[128,32]{0,1:T(8,128)S(1)} %get-tuple-element.21, f32[512,128,32]{1,0,2:T(8,128)S(1)} %get-tuple-element.22, pred[128,512]{0,1:T(8,128)(4,1)S(1)} %fusion.34, ...), kind=kOutput, calls=%fused_computation.9 | convolution fusion | flops 2164260864 | bytes 25804800 | tf_op jit(solution)/shard_map/thj,kj->thk/dot_general | solution.py:52
  69.6 2.0 copy-done.2
  71.6 8.3 %fusion.30 = f32[512,512]{1,0:T(8,128)} fusion(f32[512,512]{1,0:T(8,128)S(1)} %fusion.22, bf16[128,32,512]{0,2,1:T(8,128)(2,1)S(1)} %get-tuple-element.23, bf16[128,32,512]{2,1,0:T(8,128)(2,1)} %param.7), kind=kOutput, calls=%fused_computation.30 | convolution fusion | flops 2147745792 | bytes 10485760 | tf_op jit(solution)/shard_map/thk,thj->kj/dot_general | solution.py:59
  79.9 0.2 fusion.36
  80.1 28.2 %reduce-scatter.4.cloned.1.call-done = f32[4,32,512]{2,1,0:T(8,128)} async-done(((f32[4,128,512]{2,1,0:T(8,128)}), f32[4,32,512]{2,1,0:T(8,128)}) %reduce-scatter.4.cloned.1.call-update) | async-done | bytes 262160 | tf_op jit(solution)/shard_map/reduce_scatter | solution.py:66
  108.3 0.9 slice_bitcast_fusion.2
  109.2 1.3 collective-permute-start.6
  110.5 1.3 collective-permute-start.7
  111.8 1.3 collective-permute-start.8
  113.1 8.7 %fusion.2 = bf16[512,32,128]{2,0,1:T(8,128)(2,1)} fusion(f32[512,128,32]{1,0,2:T(8,128)} %get-tuple-element.24, f32[512,128,32]{1,0,2:T(8,128)} %copy-done.1, f32[32,128]{1,0:T(8,128)S(1)} %bitcast.123, f32[32,128]{1,0:T(8,128)S(1)} %bitcast.122, f32[32,128]{1,0:T(8,128)S(1)} %bitcast.121, pred[512,128]{1,0:T(8,128)(4,1)S(1)} %fusion.36), kind=kLoop, calls=%fused_computation.3 | loop fusion | flops 14680064 | bytes 21086208 | tf_op jit(solution)/shard_map/convert_element_type | solution.py:53
  121.8 0.9 fusion.40
  122.7 0.7 stack.2
  123.4 3.3 %all-to-all-start = ((bf16[4,32,512]{2,1,0:T(8,128)(2,1)}), bf16[4,32,512]{2,1,0:T(8,128)(2,1)S(1)}, u32[]{:S(2)}, u32[]{:S(2)}) async-start(bf16[4,32,512]{2,1,0:T(8,128)(2,1)} %stack.2), calls=%async_computation.1 | async-start | bytes 262144 | tf_op jit(solution)/shard_map/all_to_all | solution.py:79
  126.7 0.0 reduce-scatter.6.cloned.1.call-start
  126.8 4.1 %convolution_bitcast_fusion = f32[4,128,64]{2,1,0:T(8,128)} fusion(bf16[4,128,32,128]{3,1,0,2:T(8,128)(2,1)} %bitcast.114, bf16[128,32,64,1]{0,2,3,1:T(8,128)(2,1)S(1)} %bitcast.116), kind=kOutput, calls=%fused_computation.32 | convolution fusion | flops 268435456 | bytes 4849664 | tf_op jit(solution)/shard_map/thk,thr->kr/dot_general | solution.py:62
  130.9 0.0 reduce-scatter.8.cloned.1.call-start
  130.9 0.9 all-to-all-done
  131.9 2.4 %fusion.50 = f32[512,1792]{1,0:T(8,128)} fusion(bf16[128,512]{1,0:T(8,128)(2,1)S(1)} %bitcast.118, bf16[128,1792]{1,0:T(8,128)(2,1)S(1)} %copy-done), kind=kOutput, calls=%fused_computation.64 | convolution fusion | flops 234881024 | bytes 4259840 | tf_op jit(solution)/shard_map/dot_general | solution.py:87
  134.4 6.5 %convolution_convert_fusion = bf16[128,32,512]{2,0,1:T(8,128)(2,1)} fusion(bf16[128,32,512]{0,2,1:T(8,128)(2,1)} %copy-done.2, bf16[128,512]{1,0:T(8,128)(2,1)S(1)} %copy-done.3, bf16[128,512]{1,0:T(8,128)(2,1)S(1)} %collective-permute-done.2, bf16[128,512]{1,0:T(8,128)(2,1)S(1)} %collective-permute-done.1, bf16[128,512]{1,0:T(8,128)(2,1)S(1)} %collective-permute-done), kind=kOutput, calls=%fused_computation.25 | convolution fusion | flops 2151677952 | bytes 8912896 | tf_op jit(solution)/shard_map/thk,kj->thj/dot_general | solution.py:54
  140.9 18.6 %reduce-scatter.6.cloned.1.call-done = f32[4,32,64]{2,1,0:T(8,128)} async-done(((f32[4,128,64]{2,1,0:T(8,128)}), f32[4,32,64]{2,1,0:T(8,128)}) %reduce-scatter.6.cloned.1.call-update) | async-done | bytes 32784 | tf_op jit(solution)/shard_map/reduce_scatter | solution.py:67
  159.5 0.8 slice_bitcast_fusion.6
  160.2 1.3 collective-permute-start.10
  161.5 1.3 collective-permute-start.11
  162.8 1.6 collective-permute-start.9
  164.4 3.0 %convolution_convert_fusion.1 = bf16[128,32,64]{0,2,1:T(8,128)(2,1)S(1)} fusion(bf16[128,32,512]{0,2,1:T(8,128)(2,1)} %copy-done.2, bf16[128,64]{0,1:T(8,128)(2,1)S(1)} %copy-done.4, bf16[128,64]{0,1:T(8,128)(2,1)S(1)} %collective-permute-done.5, bf16[128,64]{0,1:T(8,128)(2,1)S(1)} %collective-permute-done.4, bf16[128,64]{0,1:T(8,128)(2,1)S(1)} %collective-permute-done.3), kind=kOutput, calls=%fused_computation.31 | convolution fusion | flops 268959744 | bytes 4784128 | tf_op jit(solution)/shard_map/thk,kr->thr/dot_general | solution.py:57
  167.4 6.9 %copy.36 = bf16[128,32,512]{2,1,0:T(8,128)(2,1)} copy(bf16[128,32,512]{2,0,1:T(8,128)(2,1)} %convolution_convert_fusion) | data formatting | bytes 8388608
  174.3 1.0 copy.37
  175.3 0.7 fusion.45
  176.0 8.2 %all_gather.3 = bf16[128,64]{1,0:T(8,128)(2,1)S(1)} all-gather(bf16[32,64]{1,0:T(8,128)(2,1)S(1)} %fusion.45), channel_id=1, replica_groups=mesh['ctx'=8,'head'=4] {'head'}, dimensions={0}, use_global_device_ids=true | all-gather | bytes 20480 | tf_op jit(solution)/shard_map/all_gather | solution.py:84
  184.2 0.7 copy.38
  184.9 22.7 %reduce-scatter.8.cloned.1.call-done = f32[64,1792]{1,0:T(8,128)} async-done(((f32[512,1792]{1,0:T(8,128)}), f32[64,1792]{1,0:T(8,128)}) %reduce-scatter.8.cloned.1.call-update) | async-done | bytes 458768 | tf_op jit(solution)/shard_map/reduce_scatter | solution.py:86
  207.6 0.7 copy.66
  (26 shorter events, 0.1 us)
Async XLA Ops:
  7.2 124.7 %copy-start = (bf16[128,1792]{1,0:T(8,128)(2,1)S(1)}, bf16[128,1792]{1,0:T(8,128)(2,1)}, u32[]{:S(2)}) copy-start(bf16[128,1792]{1,0:T(8,128)(2,1)} %param.12) | copy-start | bytes 1376260
  7.2 22.3 %copy-start.3 = (bf16[128,512]{1,0:T(8,128)(2,1)S(1)}, bf16[128,512]{1,0:T(8,128)(2,1)}, u32[]{:S(2)}) copy-start(bf16[128,512]{1,0:T(8,128)(2,1)} %param.9) | copy-start | bytes 393220
  7.2 101.1 %reduce-scatter.4.cloned.1.call-start = ((), (), s32[]{:S(2)}) async-start(), calls=%async_computation.4 | async-start | bytes 1310720 | tf_op jit(solution)/shard_map/reduce_scatter | solution.py:66
  7.2 18.0 %collective-permute-start.3 = (bf16[128,64]{0,1:T(8,128)(2,1)}, bf16[128,64]{0,1:T(8,128)(2,1)S(1)}, u32[]{:S(2)}, u32[]{:S(2)}) collective-permute-start(bf16[128,64]{0,1:T(8,128)(2,1)} %param.10), channel_id=1, source_target_pairs={{0,12},{4,16},{8,20},{12,24},{16,28},{1,13},{5,17},{9,21},{13,25},... | collective-permute-start | bytes 49160 | tf_op jit(solution)/shard_map/ppermute | solution.py:13
  11.8 15.7 %collective-permute-start.4 = (bf16[128,64]{0,1:T(8,128)(2,1)}, bf16[128,64]{0,1:T(8,128)(2,1)S(1)}, u32[]{:S(2)}, u32[]{:S(2)}) collective-permute-start(bf16[128,64]{0,1:T(8,128)(2,1)} %param.10), channel_id=1, source_target_pairs={{0,8},{4,12},{8,16},{12,20},{16,24},{20,28},{1,9},{5,13},{9,17},{1... | collective-permute-start | bytes 49160 | tf_op jit(solution)/shard_map/ppermute | solution.py:13
  15.3 12.2 %collective-permute-start.5 = (bf16[128,64]{0,1:T(8,128)(2,1)}, bf16[128,64]{0,1:T(8,128)(2,1)S(1)}, u32[]{:S(2)}, u32[]{:S(2)}) collective-permute-start(bf16[128,64]{0,1:T(8,128)(2,1)} %param.10), channel_id=1, source_target_pairs={{0,4},{4,8},{8,12},{12,16},{16,20},{20,24},{24,28},{1,5},{5,9},{9,... | collective-permute-start | bytes 49160 | tf_op jit(solution)/shard_map/ppermute | solution.py:13
  18.6 10.9 %collective-permute-start = (bf16[128,512]{1,0:T(8,128)(2,1)}, bf16[128,512]{1,0:T(8,128)(2,1)S(1)}, u32[]{:S(2)}, u32[]{:S(2)}) collective-permute-start(bf16[128,512]{1,0:T(8,128)(2,1)} %param.9), channel_id=1, source_target_pairs={{0,12},{4,16},{8,20},{12,24},{16,28},{1,13},{5,17},{9,21},{13,25},... | collective-permute-start | bytes 393224 | tf_op jit(solution)/shard_map/ppermute | solution.py:13
  20.4 9.1 %collective-permute-start.1 = (bf16[128,512]{1,0:T(8,128)(2,1)}, bf16[128,512]{1,0:T(8,128)(2,1)S(1)}, u32[]{:S(2)}, u32[]{:S(2)}) collective-permute-start(bf16[128,512]{1,0:T(8,128)(2,1)} %param.9), channel_id=1, source_target_pairs={{0,8},{4,12},{8,16},{12,20},{16,24},{20,28},{1,9},{5,13},{9,17},{1... | collective-permute-start | bytes 393224 | tf_op jit(solution)/shard_map/ppermute | solution.py:13
  25.2 4.3 %collective-permute-start.2 = (bf16[128,512]{1,0:T(8,128)(2,1)}, bf16[128,512]{1,0:T(8,128)(2,1)S(1)}, u32[]{:S(2)}, u32[]{:S(2)}) collective-permute-start(bf16[128,512]{1,0:T(8,128)(2,1)} %param.9), channel_id=1, source_target_pairs={{0,4},{4,8},{8,12},{12,16},{16,20},{20,24},{24,28},{1,5},{5,9},{9,... | collective-permute-start | bytes 393224 | tf_op jit(solution)/shard_map/ppermute | solution.py:13
  39.1 20.3 %copy-start.1 = (f32[512,128,32]{1,0,2:T(8,128)}, f32[512,128,32]{1,0,2:T(8,128)S(1)}, u32[]{:S(2)}) copy-start(f32[512,128,32]{1,0,2:T(8,128)S(1)} %get-tuple-element.22) | copy-start | bytes 25165828
  39.1 5.2 %copy-start.5 = (bf16[128,32,512]{2,1,0:T(8,128)(2,1)S(1)}, bf16[128,32,512]{2,1,0:T(8,128)(2,1)}, u32[]{:S(2)}) copy-start(bf16[128,32,512]{2,1,0:T(8,128)(2,1)} %param.11) | copy-start | bytes 12582916
  69.6 2.0 copy-start.2
  109.2 12.6 %collective-permute-start.6 = (f32[32,512]{1,0:T(8,128)S(1)}, f32[32,512]{1,0:T(8,128)S(1)}, u32[]{:S(2)}, u32[]{:S(2)}) collective-permute-start(f32[32,512]{1,0:T(8,128)S(1)} %get-tuple-element.15), channel_id=1, source_target_pairs={{4,0},{8,4},{12,8},{16,12},{20,16},{24,20},{28,24},{5,1},{9,5},{13... | collective-permute-start | bytes 196616 | tf_op jit(solution)/shard_map/ppermute | solution.py:13
  110.5 11.3 %collective-permute-start.7 = (f32[32,512]{1,0:T(8,128)S(1)}, f32[32,512]{1,0:T(8,128)S(1)}, u32[]{:S(2)}, u32[]{:S(2)}) collective-permute-start(f32[32,512]{1,0:T(8,128)S(1)} %get-tuple-element.17), channel_id=1, source_target_pairs={{8,0},{12,4},{16,8},{20,12},{24,16},{28,20},{9,1},{13,5},{17,9},{2... | collective-permute-start | bytes 196616 | tf_op jit(solution)/shard_map/ppermute | solution.py:13
  111.8 10.0 %collective-permute-start.8 = (f32[32,512]{1,0:T(8,128)S(1)}, f32[32,512]{1,0:T(8,128)S(1)}, u32[]{:S(2)}, u32[]{:S(2)}) collective-permute-start(f32[32,512]{1,0:T(8,128)S(1)} %get-tuple-element.16), channel_id=1, source_target_pairs={{12,0},{16,4},{20,8},{24,12},{28,16},{13,1},{17,5},{21,9},{25,13},... | collective-permute-start | bytes 196616 | tf_op jit(solution)/shard_map/ppermute | solution.py:13
  123.4 8.5 %all-to-all-start = ((bf16[4,32,512]{2,1,0:T(8,128)(2,1)}), bf16[4,32,512]{2,1,0:T(8,128)(2,1)S(1)}, u32[]{:S(2)}, u32[]{:S(2)}) async-start(bf16[4,32,512]{2,1,0:T(8,128)(2,1)} %stack.2), calls=%async_computation.1 | async-start | bytes 262144 | tf_op jit(solution)/shard_map/all_to_all | solution.py:79
  126.7 32.8 %reduce-scatter.6.cloned.1.call-start = ((), (), s32[]{:S(2)}) async-start(), calls=%async_computation.5 | async-start | bytes 327680 | tf_op jit(solution)/shard_map/reduce_scatter | solution.py:67
  130.9 76.7 %reduce-scatter.8.cloned.1.call-start = ((), (), s32[]{:S(2)}) async-start(), calls=%async_computation.6 | async-start | bytes 4128768 | tf_op jit(solution)/shard_map/reduce_scatter | solution.py:86
  131.9 32.5 %copy-start.4 = (bf16[128,64]{0,1:T(8,128)(2,1)S(1)}, bf16[128,64]{0,1:T(8,128)(2,1)}, u32[]{:S(2)}) copy-start(bf16[128,64]{0,1:T(8,128)(2,1)} %param.10) | copy-start | bytes 49156
  160.2 15.1 %collective-permute-start.10 = (f32[32,64]{1,0:T(8,128)S(1)}, f32[32,64]{1,0:T(8,128)S(1)}, u32[]{:S(2)}, u32[]{:S(2)}) collective-permute-start(f32[32,64]{1,0:T(8,128)S(1)} %get-tuple-element.20), channel_id=1, source_target_pairs={{8,0},{12,4},{16,8},{20,12},{24,16},{28,20},{9,1},{13,5},{17,9},{2... | collective-permute-start | bytes 24584 | tf_op jit(solution)/shard_map/ppermute | solution.py:13
  161.5 13.8 %collective-permute-start.11 = (f32[32,64]{1,0:T(8,128)S(1)}, f32[32,64]{1,0:T(8,128)S(1)}, u32[]{:S(2)}, u32[]{:S(2)}) collective-permute-start(f32[32,64]{1,0:T(8,128)S(1)} %get-tuple-element.19), channel_id=1, source_target_pairs={{12,0},{16,4},{20,8},{24,12},{28,16},{13,1},{17,5},{21,9},{25,13},... | collective-permute-start | bytes 24584 | tf_op jit(solution)/shard_map/ppermute | solution.py:13
  162.8 12.5 %collective-permute-start.9 = (f32[32,64]{1,0:T(8,128)S(1)}, f32[32,64]{1,0:T(8,128)S(1)}, u32[]{:S(2)}, u32[]{:S(2)}) collective-permute-start(f32[32,64]{1,0:T(8,128)S(1)} %get-tuple-element.18), channel_id=1, source_target_pairs={{4,0},{8,4},{12,8},{16,12},{20,16},{24,20},{28,24},{5,1},{9,5},{13... | collective-permute-start | bytes 24584 | tf_op jit(solution)/shard_map/ppermute | solution.py:13
Sparse Core Ops, SparseCore 0:
  80.0 28.2 reduce-scatter.3
  131.0 28.4 reduce-scatter.5
  162.4 45.2 reduce-scatter.7
